TPU v7x, 32 devices: a whole 2x2x4 slice. The times are simulated.
32 devices in a mesh: dp: 8 (over z, x), expert: 4 (over y, core).
Axes of the slice: x: 2, y: 2, z: 4, core: 2. Of those that a mesh axis runs over, the one named last changes fastest.
Arguments:
- tokens: bfloat16 [4096, 2048], P(('dp', 'expert')), may hold values from -6 to 6
- cotangent: bfloat16 [4096, 2048], P(('dp', 'expert')), may hold values from -6 to 6
- expert_ids: int32 [4096, 2], P(('dp', 'expert')), may hold values from 0 to 3, all different within a row; in each aligned block of 128 rows (0 to 127, 128 to 255, ...) at most 72 rows name the same one
- route_share: float32 [4096], P(('dp', 'expert')), may hold values from 0.5 to 0.95
- gate_proj: bfloat16 [4, 7168, 2048], P('expert', 'dp'), may hold values from -0.125 to 0.125
- up_proj: bfloat16 [4, 7168, 2048], P('expert', 'dp'), may hold values from -0.125 to 0.125
- down_anchor: float32 [4, 7168, 2048], P('expert', 'dp'), may hold values from -0.12 to 0.12
- down_average: float32 [4, 7168, 2048], P('expert', 'dp'), may hold values from -0.12 to 0.12
- down_moment: float32 [4, 7168, 2048], P('expert', 'dp'), may hold values from 0.002 to 0.05
Outputs:
- new_anchor: float32 [4, 7168, 2048], P('expert', 'dp')
- new_average: float32 [4, 7168, 2048], P('expert', 'dp')
- new_moment: float32 [4, 7168, 2048], P('expert', 'dp')
Inputs may be any that keep to these rules, and one draw needn't show every extreme that they name: `expert_ids`: the two ids of a token differ. The rows of one device name any expert at most 72 times, and in every draw some device names some expert exactly 72 times.
All inputs are finite; a program needn't handle non-finite values.
Results may differ from a plain program's by a relative error of at most 0.0043.
Values may be sent and summed in bfloat16 or wider, within the bound.
A program may use at most 192 MiB of HBM per device.

v0:
```python
import jax
import jax.numpy as jnp
from jax import lax
from jax.sharding import PartitionSpec as P

FF = 7168
TOPK = 2


beta_one = 0.9
beta_two = 0.95
learn_rate = 0.05
decay_rate = 0.1
step_count = 4.0
epsilon = 1e-08


def expert_terms(pieces, weight_gate, weight_up):
    rows_in, gated_rows = pieces
    gate_act = lax.dot_general(
        rows_in, weight_gate, (((1,), (1,)), ((), ())), preferred_element_type=jnp.float32
    )
    up_act = lax.dot_general(
        rows_in, weight_up, (((1,), (1,)), ((), ())), preferred_element_type=jnp.float32
    )
    hidden = (jax.nn.silu(gate_act) * up_act).astype(jnp.bfloat16)
    return lax.dot_general(
        hidden, gated_rows, (((0,), (0,)), ((), ())), preferred_element_type=jnp.float32
    )


def shards(
    tokens,
    cotangent,
    expert_ids,
    route_share,
    gate_proj,
    up_proj,
    down_anchor,
    down_average,
    down_moment,
):
    experts_all = lax.axis_size("expert")
    tok_rows = tokens.shape[0]
    width = tokens.shape[1]
    capacity = tok_rows * TOPK // experts_all * 9 // 8
    slots = experts_all * capacity
    shares = jnp.stack([route_share, 1.0 - route_share], axis=1)
    expert_range = jnp.arange(experts_all, dtype=jnp.int32)
    flat_ids = expert_ids.reshape(-1)
    onehot_routes = (flat_ids[:, None] == expert_range[None, :]).astype(jnp.int32)
    earlier = jnp.cumsum(onehot_routes, axis=0) - onehot_routes
    slot_of = jnp.sum(earlier * onehot_routes, axis=1)
    target = (flat_ids * capacity + slot_of).reshape(tok_rows, TOPK)
    slot_range = jnp.arange(slots, dtype=jnp.int32)
    placed = target[None, :, :] == slot_range[:, None, None]
    picker = jnp.sum(placed.astype(jnp.float32), axis=2).astype(jnp.bfloat16)
    slot_share = jnp.sum(jnp.where(placed, shares[None, :, :], 0.0), axis=(1, 2))
    send_rows = jnp.dot(picker, tokens, preferred_element_type=jnp.float32).astype(jnp.bfloat16)
    send_grad = (
        slot_share[:, None] * jnp.dot(picker, cotangent, preferred_element_type=jnp.float32)
    ).astype(jnp.bfloat16)
    weight_gate = gate_proj[0]
    weight_up = up_proj[0]
    arrived = (
        lax.all_to_all(
            send_rows.reshape(experts_all, capacity, width),
            "expert",
            split_axis=0,
            concat_axis=0,
            tiled=True,
        ),
        lax.all_to_all(
            send_grad.reshape(experts_all, capacity, width),
            "expert",
            split_axis=0,
            concat_axis=0,
            tiled=True,
        ),
    )
    rows_here = arrived[0].reshape(slots, width)
    grad_here = arrived[1].reshape(slots, width)
    gradient = expert_terms(
        (
            lax.all_gather(rows_here, "dp", axis=0, tiled=True),
            lax.all_gather(grad_here, "dp", axis=0, tiled=True),
        ),
        weight_gate,
        weight_up,
    )
    gradient = gradient[None] * FF ** (-0.5)
    bias_two = 1.0 - beta_two**step_count
    eval_point = (1.0 - beta_one) * down_anchor + beta_one * down_average
    second_moment = beta_two * down_moment + (1.0 - beta_two) * gradient * gradient
    update_dir = gradient / (jnp.sqrt(second_moment / bias_two) + epsilon) + decay_rate * eval_point
    new_anchor = down_anchor - learn_rate * update_dir
    new_average = (1.0 - 1.0 / step_count) * down_average + 1.0 / step_count * new_anchor
    return (new_anchor, new_average, second_moment)


def solution(mesh):
    placed = (
        P(("dp", "expert"), None),
        P(("dp", "expert"), None),
        P(("dp", "expert"), None),
        P(("dp", "expert")),
        P("expert", "dp", None),
        P("expert", "dp", None),
        P("expert", "dp", None),
        P("expert", "dp", None),
        P("expert", "dp", None),
    )
    return jax.shard_map(
        shards,
        mesh=mesh,
        in_specs=placed,
        out_specs=(P("expert", "dp", None), P("expert", "dp", None), P("expert", "dp", None)),
        check_vma=False,
    )
```

profile of v0, /device:TPU:0, one launch (start us, length us, event | category | flops | bytes accessed | tf_op | source)
XLA Modules:
  0.0 372.1 jit_solution(6076371271593969751)
XLA Ops:
  7.2 0.0 copy-start
  7.2 0.0 all-gather.3.cloned.1.call-start
  7.2 0.8 copy.30
  8.1 0.1 eq.42
  8.2 0.1 eq.38
  8.3 0.7 subtract_bitcast_fusion
  9.0 1.2 reduce-window.6
  10.2 0.1 slice.8
  10.3 0.1 copy.32
  10.4 0.1 copy.33
  10.5 0.1 add_bitcast_fusion
  10.6 0.1 reduce_sum.30
  10.8 0.1 copy.34
  10.8 0.7 multiply_add_fusion.1
  11.5 0.7 pad_maximum_fusion
  12.2 0.2 convert_reduce_fusion
  12.4 0.0 copy-done
  12.4 0.5 convolution_convert_fusion
  12.8 20.0 %all_to_all.10 = bf16[4,72,2048]{2,1,0:T(8,128)(2,1)} all-to-all(bf16[4,72,2048]{2,1,0:T(8,128)(2,1)S(1)} %bitcast.57), channel_id=1, replica_groups=mesh['dp'=8,'expert'=4] {'expert'}, dimensions={0} | all-to-all | bytes 2359296 | tf_op jit(solution)/shard_map/all_to_all | solution.py:66
  32.8 0.0 all-gather.3.cloned.1.call-update
  32.9 0.0 all-gather.5.cloned.1.call-start
  32.9 1.5 fusion.9
  34.4 19.0 %all_to_all.11 = bf16[4,72,2048]{2,1,0:T(8,128)(2,1)} all-to-all(bf16[4,72,2048]{2,1,0:T(8,128)(2,1)S(1)} %bitcast.56), channel_id=1, replica_groups=mesh['dp'=8,'expert'=4] {'expert'}, dimensions={0} | all-to-all | bytes 2359296 | tf_op jit(solution)/shard_map/all_to_all | solution.py:73
  53.4 0.0 all-gather.5.cloned.1.call-update
  53.4 117.6 %all-gather.3.cloned.1.call-done = bf16[2304,2048]{1,0:T(8,128)(2,1)} async-done(((bf16[288,2048]{1,0:T(8,128)(2,1)}), bf16[2304,2048]{1,0:T(8,128)(2,1)}) %all-gather.3.cloned.1.call-update) | async-done | bytes 9437200 | tf_op jit(solution)/shard_map/all_gather | solution.py:85
  171.0 15.7 %fusion.7 = f32[2304,896]{1,0:T(8,128)} fusion(bf16[2304,2048]{1,0:T(8,128)(2,1)} %all-gather.3.cloned.1.call-done, bf16[1,896,2048]{2,1,0:T(8,128)(2,1)} %param.13), kind=kOutput, calls=%fused_computation.10 | convolution fusion | flops 8455716864 | bytes 21364736 | tf_op jit(solution)/shard_map/dot_general | solution.py:20
  186.7 121.9 %all-gather.5.cloned.1.call-done = bf16[2304,2048]{1,0:T(8,128)(2,1)} async-done(((bf16[288,2048]{1,0:T(8,128)(2,1)}), bf16[2304,2048]{1,0:T(8,128)(2,1)}) %all-gather.5.cloned.1.call-update) | async-done | bytes 9437200 | tf_op jit(solution)/shard_map/all_gather | solution.py:86
  308.7 0.0 copy-start.1
  308.7 56.5 %multiply_add_fusion = (f32[1,896,2048]{2,1,0:T(8,128)}, f32[1,896,2048]{2,1,0:T(8,128)}, f32[1,896,2048]{2,1,0:T(8,128)}) fusion(f32[1,896,2048]{2,1,0:T(8,128)} %param.16, f32[1,896,2048]{2,1,0:T(8,128)} %param.15, f32[1,896,2048]{2,1,0:T(8,128)} %param.17, bf16[2304,2048]{1,0:T(8,128)(2,1)} %all-gather.5.cloned.1.call-done, f32[2304,896]{1,0:T(8,128)} %fusion.7, ...), kind=kOutput, calls=%fused_computation.6 | convolution fusion | flops 16956850176 | bytes 74842112 | tf_op jit(solution)/shard_map/dot_general | solution.py:27
  365.2 0.0 copy-done.1
  (4 shorter events, 0.1 us)
Async XLA Ops:
  7.2 5.2 %copy-start = (bf16[128,2048]{1,0:T(8,128)(2,1)S(1)}, bf16[128,2048]{1,0:T(8,128)(2,1)}, u32[]{:S(2)}) copy-start(bf16[128,2048]{1,0:T(8,128)(2,1)} %param.9) | copy-start | bytes 1572868
  7.2 163.8 %all-gather.3.cloned.1.call-start = ((), (), s32[]{:S(2)}) async-start(), calls=%async_computation.2 | async-start | bytes 10616832 | tf_op jit(solution)/shard_map/all_gather | solution.py:85
  32.9 275.8 %all-gather.5.cloned.1.call-start = ((), (), s32[]{:S(2)}) async-start(), calls=%async_computation.3 | async-start | bytes 10616832 | tf_op jit(solution)/shard_map/all_gather | solution.py:86
  308.7 56.5 %copy-start.1 = (bf16[128,2048]{1,0:T(8,128)(2,1)S(1)}, bf16[128,2048]{1,0:T(8,128)(2,1)}, u32[]{:S(2)}) copy-start(bf16[128,2048]{1,0:T(8,128)(2,1)} %param.9) | copy-start | bytes 1572868
Sparse Core Ops, SparseCore 0:
  33.0 137.9 all-gather.2
  173.2 135.4 all-gather.4
where the time goes:
time: 372 us
  waiting for transfers between devices  240 us (65%)
  matrix products  74.2 us (20%)
  blocking collectives  39 us (10%)
  between operations  14.1 us (4%)
    all_gather x1, waiting for transfers between devices, shards(): lax.all_gather(grad_here, 'dp', axis=0, tiled=True)  122 us
    all_gather x1, waiting for transfers between devices, shards(): lax.all_gather(rows_here, 'dp', axis=0, tiled=True)  118 us
    dot_general x1, matrix products, expert_terms(): lax.dot_general(hidden, gated_rows, (((0,), (0,)), ((), ())), preferred_e...  56.5 us
    all_to_all x1, blocking collectives, shards(): lax.all_to_all(send_rows.reshape(experts_all, capacity, width), 'expert',...  20 us
    all_to_all x1, blocking collectives, shards(): lax.all_to_all(send_grad.reshape(experts_all, capacity, width), 'expert',...  19 us
    dot_general x1, matrix products, expert_terms(): lax.dot_general(rows_in, weight_gate, (((1,), (1,)), ((), ())), preferred...  15.7 us
  transfers between devices with their start and end apart: 2, of which 2 were waited for; matrix products, arithmetic and copies ran while one was open for 5% of the time, Pallas kernels for 0%

commit v1 on v0

--- a/solution.py
+++ b/solution.py
@@ -29,7 +29,7 @@
     )
 
 
-def shards(
+def routed_shards(
     tokens,
     cotangent,
     expert_ids,
@@ -98,6 +98,49 @@
     return (new_anchor, new_average, second_moment)
 
 
+def adam(gradient, down_anchor, down_average, down_moment):
+    bias_two = 1.0 - beta_two**step_count
+    eval_point = (1.0 - beta_one) * down_anchor + beta_one * down_average
+    second_moment = beta_two * down_moment + (1.0 - beta_two) * gradient * gradient
+    update_dir = gradient / (jnp.sqrt(second_moment / bias_two) + epsilon) + decay_rate * eval_point
+    new_anchor = down_anchor - learn_rate * update_dir
+    new_average = (1.0 - 1.0 / step_count) * down_average + 1.0 / step_count * new_anchor
+    return (new_anchor, new_average, second_moment)
+
+
+def expert_shares(expert_ids, route_share, experts):
+    shares = jnp.stack([route_share, 1.0 - route_share], axis=0)
+    expert_range = jnp.arange(experts, dtype=jnp.int32)
+    named = expert_ids.T[:, None, :] == expert_range[None, :, None]
+    return jnp.sum(jnp.where(named, shares[:, None, :], 0.0), axis=0)
+
+
+def dense_shards(
+    tokens,
+    cotangent,
+    expert_ids,
+    route_share,
+    gate_proj,
+    up_proj,
+    down_anchor,
+    down_average,
+    down_moment,
+):
+    experts_all = lax.axis_size("expert")
+    axes = ("dp", "expert")
+    table = expert_shares(expert_ids, route_share, experts_all)
+    share = lax.all_gather(table, axes, axis=1, tiled=True)
+    share = lax.dynamic_index_in_dim(share, lax.axis_index("expert"), 0, keepdims=True)
+    rows = lax.all_gather(tokens, axes, axis=0, tiled=True)
+    grads = lax.all_gather(cotangent, axes, axis=0, tiled=True)
+    dims = (((1,), (1,)), ((), ()))
+    gate_act = lax.dot_general(gate_proj[0], rows, dims, preferred_element_type=jnp.float32)
+    up_act = lax.dot_general(up_proj[0], rows, dims, preferred_element_type=jnp.float32)
+    hidden = (jax.nn.silu(gate_act) * up_act * share).astype(jnp.bfloat16)
+    gradient = jnp.dot(hidden, grads, preferred_element_type=jnp.float32)
+    return adam(gradient[None] * FF ** (-0.5), down_anchor, down_average, down_moment)
+
+
 def solution(mesh):
     placed = (
         P(("dp", "expert"), None),
@@ -110,6 +153,7 @@
         P("expert", "dp", None),
         P("expert", "dp", None),
     )
+    shards = dense_shards if mesh.shape["expert"] <= 2 * TOPK else routed_shards
     return jax.shard_map(
         shards,
         mesh=mesh,

time: 372 us -> 284 us (0.76)
  waiting for transfers between devices: 240 us -> 145 us
  blocking collectives: 39 us -> 44.2 us
  matrix products: 74.2 us -> 78.8 us
    all_gather x2, waiting for transfers between devices: 240 us -> 144 us  [the longest x1 73.1 us: dense_shards(): rows = lax.all_gather(tokens, axes, axis=0, tiled=True)]
    all_gather x0 -> x1, blocking collectives: none -> 44.2 us  [dense_shards(): share = lax.all_gather(table, axes, axis=1, tiled=True)]
    all_to_all x2 -> x0, blocking collectives: 39 us -> none  [the longest x1 20 us: shards(): lax.all_to_all(send_rows.reshape(experts_all, capacity, width), 'expert',...]
    dot_general x4 -> x3, matrix products: 74.2 us -> 78.8 us  [the longest x1 33.8 us: dense_shards(): gradient = jnp.dot(hidden, grads, preferred_element_type=jnp.float32)]
  transfers between devices with their start and end apart: 2 -> 2, of which waited for: 2 -> 2; matrix products, arithmetic and copies ran while one was open for 5% -> 17% of each run, Pallas kernels for 0% -> 0%
where the time goes in v1:
time: 284 us
  waiting for transfers between devices  145 us (51%)
  matrix products  78.8 us (28%)
  blocking collectives  44.2 us (16%)
  between operations  14 us (5%)
    all_gather x1, waiting for transfers between devices, dense_shards(): rows = lax.all_gather(tokens, axes, axis=0, tiled=True)  73.1 us
    all_gather x1, waiting for transfers between devices, dense_shards(): grads = lax.all_gather(cotangent, axes, axis=0, tiled=True)  70.5 us
    all_gather x1, blocking collectives, dense_shards(): share = lax.all_gather(table, axes, axis=1, tiled=True)  44.2 us
    dot_general x1, matrix products, dense_shards(): gradient = jnp.dot(hidden, grads, preferred_element_type=jnp.float32)  33.8 us
    dot_general x1, matrix products, dense_shards(): lax.dot_general(up_proj[0], rows, dims, preferred_element_type=jnp.float32)  23.7 us
    dot_general x1, matrix products, dense_shards(): lax.dot_general(gate_proj[0], rows, dims, preferred_element_type=jnp.floa...  21.3 us
  transfers between devices with their start and end apart: 2, of which 2 were waited for; matrix products, arithmetic and copies ran while one was open for 17% of the time, Pallas kernels for 0%

profile of v1, /device:TPU:0, one launch (start us, length us, event | category | flops | bytes accessed | tf_op | source)
XLA Modules:
  0.0 284.1 jit_solution(15623975847709586878)
XLA Ops:
  7.2 0.0 all-gather.3.cloned.1.call-start
  7.2 0.7 all-gather.3.cloned.1.call-update
  7.9 0.0 all-gather.5.cloned.1.call-start
  7.9 0.7 all-gather.5.cloned.1.call-update
  8.7 0.7 subtract_bitcast_fusion
  9.3 0.7 pad_maximum_fusion
  10.0 0.7 select_reduce_fusion
  10.7 44.2 %all_gather.10 = f32[4,4096]{1,0:T(4,128)S(1)} all-gather(f32[4,128]{1,0:T(4,128)S(1)} %select_reduce_fusion), channel_id=1, replica_groups=mesh['dp'=8,'expert'=4] {'dp','expert'}, dimensions={1}, use_global_device_ids=true | all-gather | bytes 67584 | tf_op jit(solution)/shard_map/all_gather | solution.py:132
  54.9 73.1 %all-gather.3.cloned.1.call-done = bf16[4096,2048]{1,0:T(8,128)(2,1)} async-done(((bf16[128,2048]{1,0:T(8,128)(2,1)}), bf16[4096,2048]{1,0:T(8,128)(2,1)}) %all-gather.3.cloned.1.call-update) | async-done | bytes 16777232 | tf_op jit(solution)/shard_map/all_gather | solution.py:134
  128.0 0.0 copy-start
  128.0 21.3 %fusion.4 = f32[896,4096]{1,0:T(8,128)} fusion(bf16[4096,2048]{1,0:T(8,128)(2,1)} %all-gather.3.cloned.1.call-done, bf16[1,896,2048]{2,1,0:T(8,128)(2,1)} %param.13), kind=kOutput, calls=%fused_computation.8 | convolution fusion | flops 15032385536 | bytes 35127296 | tf_op jit(solution)/shard_map/dot_general | solution.py:137
  149.3 0.0 copy-done
  149.3 23.7 %multiply_convert_fusion = bf16[896,4096]{1,0:T(8,128)(2,1)} fusion(f32[896,4096]{1,0:T(8,128)} %fusion.4, bf16[4096,2048]{1,0:T(8,128)(2,1)} %all-gather.3.cloned.1.call-done, f32[4096]{0:T(1024)S(1)} %bitcast.27, bf16[1,896,2048]{2,1,0:T(8,128)(2,1)S(1)} %copy-done), kind=kOutput, calls=%fused_computation | convolution fusion | flops 15058075648 | bytes 42483712 | tf_op jit(solution)/shard_map/dot_general | solution.py:138
  173.0 70.5 %all-gather.5.cloned.1.call-done = bf16[4096,2048]{1,0:T(8,128)(2,1)} async-done(((bf16[128,2048]{1,0:T(8,128)(2,1)}), bf16[4096,2048]{1,0:T(8,128)(2,1)}) %all-gather.5.cloned.1.call-update) | async-done | bytes 16777232 | tf_op jit(solution)/shard_map/all_gather | solution.py:135
  243.5 33.8 %multiply_add_fusion = (f32[1,896,2048]{2,1,0:T(8,128)}, f32[1,896,2048]{2,1,0:T(8,128)}, f32[1,896,2048]{2,1,0:T(8,128)}) fusion(f32[1,896,2048]{2,1,0:T(8,128)} %param.16, f32[1,896,2048]{2,1,0:T(8,128)} %param.15, f32[1,896,2048]{2,1,0:T(8,128)} %param.17, bf16[896,4096]{1,0:T(8,128)(2,1)} %multiply_convert_fusion, ...), kind=kOutput, calls=%fused_computation.6 | convolution fusion | flops 15065415680 | bytes 68157440 | tf_op jit(solution)/shard_map/dot_general | solution.py:140
  (1 shorter events, 0.0 us)
Async XLA Ops:
  7.2 120.8 %all-gather.3.cloned.1.call-start = ((), (), s32[]{:S(2)}) async-start(), calls=%async_computation | async-start | bytes 17301504 | tf_op jit(solution)/shard_map/all_gather | solution.py:134
  7.9 235.6 %all-gather.5.cloned.1.call-start = ((), (), s32[]{:S(2)}) async-start(), calls=%async_computation.1 | async-start | bytes 17301504 | tf_op jit(solution)/shard_map/all_gather | solution.py:135
  128.0 21.3 %copy-start = (bf16[1,896,2048]{2,1,0:T(8,128)(2,1)S(1)}, bf16[1,896,2048]{2,1,0:T(8,128)(2,1)}, u32[]{:S(2)}) copy-start(bf16[1,896,2048]{2,1,0:T(8,128)(2,1)} %param.14) | copy-start | bytes 11010052
Sparse Core Ops, SparseCore 0:
  10.8 117.1 all-gather.2
  130.9 112.5 all-gather.4

commit v2 on v1

--- a/solution.py
+++ b/solution.py
@@ -1,6 +1,8 @@
 import jax
 import jax.numpy as jnp
 from jax import lax
+from jax.experimental import pallas as pl
+from jax.experimental.pallas import tpu as pltpu
 from jax.sharding import PartitionSpec as P
 
 FF = 7168
@@ -115,7 +117,244 @@
     return jnp.sum(jnp.where(named, shares[:, None, :], 0.0), axis=0)
 
 
-def dense_shards(
+def gather_kernel(
+    tok_ref, cot_ref, share_ref, gate_ref, up_ref, acc_ref,
+    tok_buf, cot_buf, share_buf, gate_buf, up_buf,
+    local_sem, recv_sem, send_sem,
+):
+    rows = tok_ref.shape[0]
+    lanes_of = share_ref.shape[0]
+    dp, ex = lax.axis_index("dp"), lax.axis_index("expert")
+    layers = lax.axis_size("dp") // 2
+    z, x = dp // 2, dp % 2
+    y, core = ex // 2, ex % 2
+    lower = z < layers // 2
+    mirror = lambda v: jnp.where(lower, v, layers - 1 - v)
+    depth = mirror(z)
+    mid, end = depth == 1, depth == 0
+    inner = (jnp.where(lower, z + 1, z - 1) * 2 + x, ex)
+    outer = (jnp.where(lower, z - 1, z + 1) * 2 + x, ex)
+    over_x = (z * 2 + 1 - x, ex)
+    over_y = (dp, (1 - y) * 2 + core)
+    partner = (dp, y * 2 + 1 - core)
+    layer = (z, mirror(1 - depth), mirror(2), mirror(3))
+    OWN, X, Y, D = range(4)
+    T, C, S = range(3)
+
+    def chip_of(p, j):
+        return (layer[p] * 2 + (x + j % 2) % 2) * 2 + (y + j // 2) % 2
+
+    def slot_of(p, j, c):
+        return chip_of(p, j) * 2 + c
+
+    def place(kind, slot):
+        if kind == S:
+            return share_buf.at[pl.ds(pl.multiple_of(slot * lanes_of, lanes_of), lanes_of), :]
+        return (tok_buf, cot_buf)[kind].at[pl.ds(pl.multiple_of(slot * rows, rows), rows), :]
+
+    count = [0]
+    always, when_mid = [], []
+
+    def piece(kind, p, j, target, into):
+        slot = slot_of(p, j, core)
+        copy = pltpu.make_async_remote_copy(
+            src_ref=place(kind, slot), dst_ref=place(kind, slot),
+            send_sem=send_sem.at[count[0]], recv_sem=recv_sem.at[kind, slot],
+            device_id=target, device_id_type=pl.DeviceIdType.MESH,
+        )
+        count[0] += 1
+        into.append(copy)
+        return copy
+
+    def send(kinds, p, j, *targets):
+        for kind in kinds:
+            for target in targets:
+                piece(kind, p, j, target, always).start()
+
+    def send_mid(kinds, p, j, target):
+        copies = [piece(kind, p, j, target, when_mid) for kind in kinds]
+
+        @pl.when(mid)
+        def _():
+            for copy in copies:
+                copy.start()
+
+    def landed(kind, slot):
+        pltpu.make_async_remote_copy(
+            src_ref=place(kind, slot), dst_ref=place(kind, slot),
+            send_sem=send_sem.at[0], recv_sem=recv_sem.at[kind, slot],
+            device_id=partner, device_id_type=pl.DeviceIdType.MESH,
+        ).wait_recv()
+
+    def arrive(kinds, p, j):
+        for kind in kinds:
+            landed(kind, slot_of(p, j, core))
+            send((kind,), p, j, partner)
+
+    def arrive_if(cond, kinds, p, j, copies, then=()):
+        @pl.when(cond)
+        def _():
+            for kind, copy in zip(kinds, copies):
+                landed(kind, slot_of(p, j, core))
+                copy.start()
+            for copy in then:
+                copy.start()
+
+    def to_partner(kinds, p, j):
+        return [piece(kind, p, j, partner, always) for kind in kinds]
+
+    def to_outer(kinds, p, j):
+        return [piece(kind, p, j, outer, when_mid) for kind in kinds]
+
+    def unit(chip):
+        width = 2 * rows
+        at = pl.ds(pl.multiple_of(chip * width, width), width)
+        share = jnp.concatenate(
+            [share_buf[pl.ds((chip * 2 + c) * lanes_of + ex, 1), :] for c in range(2)], axis=1
+        )
+        tile = acc_ref.shape[0] // 2
+        dims = (((1,), (1,)), ((), ()))
+
+        @pl.loop(0, 2)
+        def _(half):
+            own = pl.ds(pl.multiple_of(half * tile, tile), tile)
+            gate = lax.dot_general(
+                gate_buf[own, :], tok_buf[at, :], dims, preferred_element_type=jnp.float32
+            )
+            up = lax.dot_general(
+                up_buf[own, :], tok_buf[at, :], dims, preferred_element_type=jnp.float32
+            )
+            hidden = (gate / (1.0 + jnp.exp(-gate)) * up * share).astype(jnp.bfloat16)
+            acc_ref[own, :] += jnp.dot(hidden, cot_buf[at, :], preferred_element_type=jnp.float32)
+
+    def compute(*units):
+        for p, j in units:
+            for kind in (T, S, C):
+                landed(kind, slot_of(p, j, 1 - core))
+        first, number = units[0], len(units)
+        if len({p for p, _ in units}) == 1:
+            base = layer[first[0]] * 4
+
+            @pl.loop(first[1], first[1] + number)
+            def _(j):
+                unit(base + (x + j % 2) % 2 * 2 + (y + j // 2) % 2)
+        else:
+            chips = [chip_of(p, j) for p, j in units]
+
+            @pl.loop(0, number)
+            def _(k):
+                unit(jnp.where(k == 0, chips[0], chips[1]))
+
+    local = [
+        pltpu.make_async_copy(src, dst, local_sem.at[k])
+        for k, (src, dst) in enumerate(
+            (
+                (tok_ref, place(T, slot_of(0, OWN, core))),
+                (share_ref, place(S, slot_of(0, OWN, core))),
+                (cot_ref, place(C, slot_of(0, OWN, core))),
+                (gate_ref, gate_buf),
+                (up_ref, up_buf),
+            )
+        )
+    ]
+    for copy in local:
+        copy.start()
+    barrier = pltpu.get_barrier_semaphore()
+    for target in (over_x, over_y, partner, inner):
+        pl.semaphore_signal(barrier, inc=1, device_id=target, device_id_type=pl.DeviceIdType.MESH)
+
+    @pl.when(mid)
+    def _():
+        pl.semaphore_signal(barrier, inc=1, device_id=outer, device_id_type=pl.DeviceIdType.MESH)
+        pl.semaphore_wait(barrier, 5)
+
+    @pl.when(end)
+    def _():
+        pl.semaphore_wait(barrier, 4)
+
+    for copy in local[:3]:
+        copy.wait()
+
+    TS, CC = (T, S), (C,)
+    for kinds in (TS, CC):
+        send(kinds, 0, OWN, over_x, over_y, inner)
+        send_mid(kinds, 0, OWN, outer)
+        send(kinds, 0, OWN, partner)
+    for copy in local[3:]:
+        copy.wait()
+
+    @pl.loop(0, acc_ref.shape[0] // 64)
+    def _(k):
+        acc_ref[pl.ds(pl.multiple_of(k * 64, 64), 64), :] = jnp.zeros((64, acc_ref.shape[1]), jnp.float32)
+
+    second = {kinds: (to_partner(kinds, 2, OWN), to_outer(kinds, 2, OWN)) for kinds in (TS, CC)}
+    third = {kinds: (to_partner(kinds, 3, OWN), to_outer(kinds, 3, OWN)) for kinds in (TS, CC)}
+    across = {kinds: (to_partner(kinds, 2, D), to_outer(kinds, 2, D)) for kinds in (TS, CC)}
+
+    arrive(TS, 0, X)
+    send(TS, 0, X, over_y)
+    arrive(TS, 0, Y)
+    arrive(TS, 1, OWN)
+    send_mid(TS, 1, OWN, inner)
+    arrive_if(mid, TS, 2, OWN, *second[TS])
+    arrive(CC, 0, Y)
+    send(CC, 0, Y, over_x)
+    arrive(CC, 0, X)
+    arrive(CC, 1, OWN)
+    send_mid(CC, 1, OWN, inner)
+    arrive_if(mid, CC, 2, OWN, *second[CC])
+    send(TS + CC, 1, OWN, over_x, over_y)
+    arrive(TS + CC, 0, D)
+    send(TS + CC, 0, D, inner)
+    send_mid(TS + CC, 0, D, outer)
+    compute((0, OWN), (0, X), (0, Y), (0, D))
+
+    for kinds in (TS, CC):
+        arrive_if(end, kinds, 2, OWN, second[kinds][0])
+        send(kinds, 2, OWN, over_x, over_y)
+    for kinds in (TS, CC):
+        arrive_if(mid, kinds, 3, OWN, *third[kinds])
+    for kinds in (TS, CC):
+        arrive(kinds, 1, X)
+        arrive(kinds, 1, Y)
+    compute((1, OWN), (1, X), (1, Y))
+
+    for kinds in (TS, CC):
+        arrive(kinds, 2, X)
+        arrive(kinds, 2, Y)
+    arrive_if(end, TS, 3, OWN, third[TS][0])
+    send(TS, 3, OWN, over_x, over_y)
+    for kinds in (TS, CC):
+        arrive_if(mid, kinds, 2, D, *across[kinds])
+    compute((2, OWN), (2, X), (2, Y))
+
+    arrive_if(end, CC, 3, OWN, third[CC][0])
+    send(CC, 3, OWN, over_x, over_y)
+    arrive(TS + CC, 1, D)
+    arrive(TS, 3, X)
+    send(TS, 3, X, over_y)
+    compute((1, D))
+    arrive(TS, 3, Y)
+    arrive(CC, 3, Y)
+    send(CC, 3, Y, over_x)
+    arrive(CC, 3, X)
+    compute((3, OWN), (3, X), (3, Y))
+
+    for kinds in (TS, CC):
+        arrive_if(end, kinds, 2, D, across[kinds][0])
+    arrive(TS + CC, 3, D)
+    compute((2, D), (3, D))
+
+    for copy in always:
+        copy.wait_send()
+
+    @pl.when(mid)
+    def _():
+        for copy in when_mid:
+            copy.wait_send()
+
+
+def relay_shards(
     tokens,
     cotangent,
     expert_ids,
@@ -127,17 +366,30 @@
     down_moment,
 ):
     experts_all = lax.axis_size("expert")
-    axes = ("dp", "expert")
-    table = expert_shares(expert_ids, route_share, experts_all)
-    share = lax.all_gather(table, axes, axis=1, tiled=True)
-    share = lax.dynamic_index_in_dim(share, lax.axis_index("expert"), 0, keepdims=True)
-    rows = lax.all_gather(tokens, axes, axis=0, tiled=True)
-    grads = lax.all_gather(cotangent, axes, axis=0, tiled=True)
-    dims = (((1,), (1,)), ((), ()))
-    gate_act = lax.dot_general(gate_proj[0], rows, dims, preferred_element_type=jnp.float32)
-    up_act = lax.dot_general(up_proj[0], rows, dims, preferred_element_type=jnp.float32)
-    hidden = (jax.nn.silu(gate_act) * up_act * share).astype(jnp.bfloat16)
-    gradient = jnp.dot(hidden, grads, preferred_element_type=jnp.float32)
+    devices = experts_all * lax.axis_size("dp")
+    rows, width = tokens.shape
+    hidden_units = gate_proj.shape[1]
+    lines = -(-experts_all // 8) * 8
+    table = expert_shares(expert_ids, route_share, lines)
+    gradient = pl.pallas_call(
+        gather_kernel,
+        out_shape=jax.ShapeDtypeStruct((hidden_units, width), jnp.float32),
+        in_specs=[pl.BlockSpec(memory_space=pl.ANY)] * 5,
+        out_specs=pl.BlockSpec(memory_space=pltpu.VMEM),
+        scratch_shapes=[
+            pltpu.VMEM((devices * rows, width), jnp.bfloat16),
+            pltpu.VMEM((devices * rows, width), jnp.bfloat16),
+            pltpu.VMEM((devices * lines, rows), jnp.float32),
+            pltpu.VMEM((hidden_units, width), jnp.bfloat16),
+            pltpu.VMEM((hidden_units, width), jnp.bfloat16),
+            pltpu.SemaphoreType.DMA((5,)),
+            pltpu.SemaphoreType.DMA((3, devices)),
+            pltpu.SemaphoreType.DMA((192,)),
+        ],
+        compiler_params=pltpu.CompilerParams(
+            collective_id=0, has_side_effects=True, vmem_limit_bytes=62 * 1024 * 1024
+        ),
+    )(tokens, cotangent, table, gate_proj[0], up_proj[0])
     return adam(gradient[None] * FF ** (-0.5), down_anchor, down_average, down_moment)
 
 
@@ -153,7 +405,8 @@
         P("expert", "dp", None),
         P("expert", "dp", None),
     )
-    shards = dense_shards if mesh.shape["expert"] <= 2 * TOPK else routed_shards
+    small = (mesh.shape["dp"], mesh.shape["expert"]) == (8, 4)
+    shards = relay_shards if small else routed_shards
     return jax.shard_map(
         shards,
         mesh=mesh,

time: 284 us -> 162 us (0.57)
  waiting for transfers between devices: 145 us -> 0 us
  Pallas kernels: 0 us -> 140 us
  matrix products: 78.8 us -> 0 us
  blocking collectives: 44.2 us -> 0 us
  other arithmetic: 2.01 us -> 21.9 us
  between operations: 14 us -> 0.64 us
    all_gather x2 -> x0, waiting for transfers between devices: 144 us -> none  [the longest x1 73.1 us: dense_shards(): rows = lax.all_gather(tokens, axes, axis=0, tiled=True)]
    pallas_call x0 -> x1, Pallas kernels: none -> 140 us  [relay_shards(): pl.pallas_call(gather_kernel, out_shape=jax.ShapeDtypeStruct((hidden_unit...]
    dot_general x3 -> x0, matrix products: 78.8 us -> none  [the longest x1 33.8 us: dense_shards(): gradient = jnp.dot(hidden, grads, preferred_element_type=jnp.float32)]
    all_gather x1 -> x0, blocking collectives: 44.2 us -> none  [dense_shards(): share = lax.all_gather(table, axes, axis=1, tiled=True)]
    add x0 -> x1, other arithmetic: none -> 19.3 us  [adam(): (1.0 - 1.0 / step_count) * down_average + 1.0 / step_count * new_anchor]
  transfers between devices with their start and end apart: 2 -> 0, of which waited for: 2 -> 0; matrix products, arithmetic and copies ran while one was open for 17% -> 0% of each run, Pallas kernels for 0% -> 0%
where the time goes in v2:
time: 162 us
  Pallas kernels  140 us (86%)
  other arithmetic  21.9 us (14%)
    pallas_call x1, Pallas kernels, relay_shards(): pl.pallas_call(gather_kernel, out_shape=jax.ShapeDtypeStruct((hidden_unit...  140 us
    add x1, other arithmetic, adam(): (1.0 - 1.0 / step_count) * down_average + 1.0 / step_count * new_anchor  19.3 us

profile of v2, /device:TPU:0, one launch (start us, length us, event | category | flops | bytes accessed | tf_op | source)
XLA Modules:
  0.0 162.2 jit_solution(4825383764465316856)
XLA Ops:
  0.6 0.7 subtract_bitcast_fusion
  1.3 0.7 pad_maximum_fusion
  2.0 1.3 select_reduce_fusion.share_ref
  3.2 139.7 %shard_map.112 = f32[896,2048]{1,0:T(8,128)} custom-call(bf16[128,2048]{1,0:T(8,128)(2,1)} %tok_ref.1, bf16[128,2048]{1,0:T(8,128)(2,1)} %cot_ref.1, f32[8,128]{1,0:T(8,128)} %select_reduce_fusion.share_ref, bf16[896,2048]{1,0:T(8,128)(2,1)} %bitcast.18, bf16[896,2048]{1,0:T(8,128)(2,1)} %bitcast.19), custom_call_target="tpu_custom_call" | custom-call | tf_op jit(solution)/shard_map/pallas_call | solution.py:374
  142.9 19.3 %multiply_add_fusion = (f32[1,896,2048]{2,1,0:T(8,128)}, f32[1,896,2048]{2,1,0:T(8,128)}, f32[1,896,2048]{2,1,0:T(8,128)}) fusion(f32[1,896,2048]{2,1,0:T(8,128)} %param.16, f32[1,896,2048]{2,1,0:T(8,128)} %param.15, f32[896,2048]{1,0:T(8,128)} %shard_map.112, f32[1,896,2048]{2,1,0:T(8,128)} %param.17), kind=kLoop, calls=%fused_computation.5 | loop fusion | flops 33030144 | bytes 51380224 | tf_op jit(solution)/shard_map/add | solution.py:109
